TPU v7x, 32 devices: a whole 2x2x4 slice. The times are simulated.
32 devices in a mesh: row: 8 (over y, x, core), col: 4 (over z).
Axes of the slice: x: 2, y: 2, z: 4, core: 2. Of those that a mesh axis runs over, the one named last changes fastest.
Arguments:
- residual: bfloat16 [8, 4, 2048, 512], P('row', 'col'), may hold values from -6 to 6
- self_tiles: bfloat16 [8, 4, 2048, 2048], P('row', 'col'), may hold values from -0.09375 to 0.09375
- side_tiles: bfloat16 [8, 4, 2048, 2048], P('row', 'col'), may hold values from -0.09375 to 0.09375
- row_cluster_basis: bfloat16 [8, 4, 2048, 32], P('row', 'col'), may hold values from -0.125 to 0.125
- column_cluster_basis: bfloat16 [8, 4, 2048, 32], P('row', 'col'), may hold values from -1 to 1
- couplings: bfloat16 [8, 4, 64, 32, 32], P('row', 'col'), may hold values from -0.1875 to 0.1875
- near_side: int32 [8, 4], P('row', 'col'), may hold values from -1 to 1
- adm_targets: int32 [8, 4, 64], P('row', 'col'), may hold values from 0 to 31, as said below
- adm_ranks: int32 [8, 4, 64], P('row', 'col'), may hold values from 8 to 32
- adm_count: int32 [8, 4], P('row', 'col'), may hold values from 1 to 64
Outputs:
- gradient: float32 [8, 4, 2048, 512], P('row', 'col')
Inputs may be any that keep to these rules, and one draw needn't show every extreme that they name: `near_side`: -1 or +1 names the cluster row before or after around the loop of 8 rows; 0 means no such tile. Each entry of adm_targets for the block row of linear index i is the linear index of a cluster other than i; slot 0 names i - 1 or i + 1, counted round the 32 clusters; targets may repeat.
All inputs are finite; a program needn't handle non-finite values.
Results may differ from a plain program's by a relative error of at most 0.0033.
Values may be sent and summed in bfloat16 or wider, within the bound.
A program may use at most 128 MiB of HBM per device.

v0:
```python
import jax
import jax.numpy as jnp
from jax import lax
from jax.sharding import PartitionSpec as P


def with_halo(block, sides, width):
    for axis, dim in sides:
        count = lax.axis_size(axis)
        forward = [(i, i + 1) for i in range(count - 1)]
        forward.append((count - 1, 0))
        backward = [(target, source) for source, target in forward]
        low = lax.ppermute(
            lax.slice_in_dim(block, block.shape[dim] - width, None, axis=dim), axis, forward
        )
        high = lax.ppermute(lax.slice_in_dim(block, 0, width, axis=dim), axis, backward)
        block = jnp.concatenate([low, block, high], axis=dim)
    return block


def contract(tile, values):
    return lax.dot_general(
        tile, values, (((0,), (0,)), ((), ())), preferred_element_type=jnp.float32
    )


def on_device(
    residual,
    self_tiles,
    side_tiles,
    row_cluster_basis,
    column_cluster_basis,
    couplings,
    near_side,
    adm_targets,
    adm_ranks,
    adm_count,
):
    slot_count = couplings.shape[2]
    rank_dimension = couplings.shape[3]
    cluster_groups = lax.axis_size("row") * lax.axis_size("col")
    local_rows = residual[0, 0]
    coefficient_table = contract(row_cluster_basis[0, 0], local_rows).astype(jnp.bfloat16)
    rank_index = jnp.arange(rank_dimension, dtype=jnp.int32)
    slot_index = jnp.arange(slot_count, dtype=jnp.int32)
    keep_mask = (rank_index[None, :] < adm_ranks[0, 0][:, None]) & (slot_index < adm_count[0, 0])[
        :, None
    ]
    keep_float = keep_mask.astype(jnp.float32)
    masked = couplings[0, 0].astype(jnp.float32) * keep_float[:, :, None] * keep_float[:, None, :]
    onehot = (
        adm_targets[0, 0][:, None] == jnp.arange(cluster_groups, dtype=jnp.int32)[None, :]
    ).astype(jnp.float32)
    coupled_blocks = lax.dot_general(
        onehot,
        masked.reshape(slot_count, rank_dimension * rank_dimension),
        (((0,), (0,)), ((), ())),
        precision=lax.Precision.HIGHEST,
        preferred_element_type=jnp.float32,
    )
    coupled_blocks = coupled_blocks.reshape(cluster_groups, rank_dimension, rank_dimension)
    padded = with_halo(residual, (("row", 0),), 1)
    side_offset = near_side[0, 0]
    neighbour = lax.dynamic_index_in_dim(padded, side_offset + 1, 0, keepdims=False)[0]
    own_part = contract(self_tiles[0, 0], local_rows)
    side_part = contract(side_tiles[0, 0], neighbour) * (side_offset != 0).astype(jnp.float32)
    received = lax.all_to_all(
        coupled_blocks, ("row", "col"), split_axis=0, concat_axis=0, tiled=True
    )
    dual_sums = jnp.einsum(
        "cab,can->bn",
        received,
        lax.all_gather(coefficient_table[None], ("row", "col"), axis=0, tiled=True).astype(
            jnp.float32
        ),
        precision=lax.Precision.HIGHEST,
    )
    dual_vector = dual_sums.astype(jnp.bfloat16)
    distant_part = jnp.dot(
        column_cluster_basis[0, 0], dual_vector, preferred_element_type=jnp.float32
    )
    gradient = own_part + side_part + distant_part
    return gradient[None, None]


def solution(mesh):
    placed = (
        P("row", "col", None, None),
        P("row", "col", None, None),
        P("row", "col", None, None),
        P("row", "col", None, None),
        P("row", "col", None, None),
        P("row", "col", None, None, None),
        P("row", "col"),
        P("row", "col", None),
        P("row", "col", None),
        P("row", "col"),
    )
    return jax.shard_map(
        on_device,
        mesh=mesh,
        in_specs=placed,
        out_specs=P("row", "col", None, None),
        check_vma=False,
    )
```

profile of v0, /device:TPU:0, one launch (start us, length us, event | category | flops | bytes accessed | tf_op | source)
XLA Modules:
  0.0 91.9 jit_solution(10351635145926286116)
XLA Ops:
  6.5 0.0 copy-start
  6.5 0.0 all-gather.3.cloned.1.call-start
  6.5 0.5 collective-permute-start
  7.0 2.9 %collective-permute-start.1 = (bf16[1,1,2048,512]{3,2,1,0:T(8,128)(2,1)}, bf16[1,1,2048,512]{3,2,1,0:T(8,128)(2,1)}, u32[]{:S(2)}, u32[]{:S(2)}) collective-permute-start(bf16[1,1,2048,512]{3,2,1,0:T(8,128)(2,1)} %param.10), channel_id=1, source_target_pairs={{4,0},{8,4},{12,8},{16,12},{20,16},{24,20},{28,24},{0,28},{5,1},{9... | collective-permute-start | bytes 6291464 | tf_op jit(solution)/shard_map/ppermute | solution.py:16
  10.0 2.8 %fusion.15 = bf16[32,512]{1,0:T(8,128)(2,1)} fusion(bf16[1,1,2048,512]{3,2,1,0:T(8,128)(2,1)} %param.10, bf16[1,1,2048,32]{2,3,1,0:T(8,128)(2,1)} %param.13), kind=kOutput, calls=%fused_computation.18 | convolution fusion | flops 67125248 | bytes 2260992 | tf_op jit(solution)/shard_map/dot_general | solution.py:22
  12.7 0.0 all-gather.3.cloned.1.call-update
  13.4 0.7 fusion.28
  14.1 1.0 %fusion.18 = f32[64,1024]{0,1:T(8,128)S(1)} fusion(bf16[1,1,64,32,32]{2,4,3,1,0:T(8,128)(2,1)} %param.15, f32[64,32]{0,1:T(8,128)S(1)} %fusion.28), kind=kLoop, calls=%fused_computation.20 | loop fusion | flops 196608 | bytes 401408 | tf_op jit(solution)/shard_map/mul | solution.py:50
  15.1 2.0 %fusion.24 = f32[32,32,32]{2,0,1:T(8,128)S(1)} fusion(f32[32,32,64]{2,1,0:T(8,128)S(1)} %bitcast.65, s32[64]{0:T(128)} %bitcast.67), kind=kOutput, calls=%fused_computation.27 | convolution fusion | flops 25169920 | bytes 393472 | tf_op jit(solution)/shard_map/dot_general | solution.py:54
  17.1 0.3 copy.14
  17.5 0.9 reshape.99
  18.4 5.6 %all-to-all-start = ((f32[32,1,1024]{2,1,0:T(1,128)}), f32[32,1,1024]{2,1,0:T(1,128)S(1)}, u32[]{:S(2)}, u32[]{:S(2)}) async-start(f32[32,1,1024]{2,1,0:T(1,128)} %reshape.99), calls=%async_computation | async-start | bytes 262144 | tf_op jit(solution)/shard_map/all_to_all | solution.py:67
  24.0 0.0 copy-done.1
  24.0 9.7 %fusion.2 = f32[2048,512]{1,0:T(8,128)} fusion(bf16[1,1,2048,2048]{3,2,1,0:T(8,128)(2,1)} %param.11, bf16[1,1,2048,512]{3,2,1,0:T(8,128)(2,1)S(1)} %copy-done.1), kind=kOutput, calls=%fused_computation.2 | convolution fusion | flops 4294967296 | bytes 14680064 | tf_op jit(solution)/shard_map/dot_general | solution.py:22
  34.4 27.0 %all-to-all-done = f32[32,1,1024]{2,1,0:T(1,128)S(1)} async-done(((f32[32,1,1024]{2,1,0:T(1,128)}), f32[32,1,1024]{2,1,0:T(1,128)S(1)}, u32[]{:S(2)}, u32[]{:S(2)}) %all-to-all-start) | async-done | bytes 131104 | tf_op jit(solution)/shard_map/all_to_all | solution.py:67
  61.4 0.6 broadcast.48
  62.0 1.0 %reduce = f32[32,1024]{1,0:T(8,128)S(1)} reduce(f32[32,1,1024]{2,1,0:T(1,128)S(1)} %all-to-all-done, f32[]{:T(128)} %broadcast.48), dimensions={1}, to_apply=%all_to_all.3.reduce_sub_computation | reduce | bytes 262148 | tf_op jit(solution)/shard_map/all_to_all | solution.py:67
  63.0 0.2 reshape.100
  63.2 6.9 %all-gather.3.cloned.1.call-done = bf16[1024,512]{1,0:T(8,128)(2,1)} async-done(((bf16[32,512]{1,0:T(8,128)(2,1)}), bf16[1024,512]{1,0:T(8,128)(2,1)}) %all-gather.3.cloned.1.call-update) | async-done | bytes 1048592 | tf_op jit(solution)/shard_map/all_gather | solution.py:73
  70.1 1.8 %fusion.14 = bf16[32,512]{1,0:T(8,128)(2,1)S(1)} fusion(f32[32,32,32]{2,1,0:T(8,128)S(1)} %reshape.100, bf16[32,32,512]{2,1,0:T(8,128)(2,1)} %bitcast.66), kind=kOutput, calls=%fused_computation.17 | convolution fusion | flops 201342976 | bytes 1212416 | tf_op jit(solution)/shard_map/cab,can->bn/dot_general | solution.py:70
  71.9 0.7 fusion.19
  72.7 0.0 collective-permute-done
  72.7 0.0 collective-permute-done.1
  72.7 12.3 %fusion.4 = f32[1,1,2048,512]{3,2,1,0:T(8,128)} fusion(f32[512,2048]{0,1:T(8,128)S(1)} %fusion.19, f32[2048,512]{1,0:T(8,128)} %fusion.2, bf16[1,1,2048,2048]{3,2,1,0:T(8,128)(2,1)} %param.12, s32[]{:T(128)S(6)} %select_n.4, bf16[1,1,2048,512]{3,2,1,0:T(8,128)(2,1)} %collective-permute-done, bf16[1,1,2048,512]{3,2,1,0:T(8,128)(2,1)S(1)} %copy-done.1, ...), kind=kOutput, calls=%fused_computation.8 | convolution fusion | flops 4300210176 | bytes 27262984 | tf_op jit(solution)/shard_map/dot_general | solution.py:22
  (3 shorter events, 0.0 us)
Async XLA Ops:
  6.5 65.4 %copy-start = (bf16[1,1,2048,32]{2,3,1,0:T(8,128)(2,1)S(1)}, bf16[1,1,2048,32]{2,3,1,0:T(8,128)(2,1)}, u32[]{:S(2)}) copy-start(bf16[1,1,2048,32]{2,3,1,0:T(8,128)(2,1)} %param.14) | copy-start | bytes 393220
  6.5 17.5 %copy-start.1 = (bf16[1,1,2048,512]{3,2,1,0:T(8,128)(2,1)S(1)}, bf16[1,1,2048,512]{3,2,1,0:T(8,128)(2,1)}, u32[]{:S(2)}) copy-start(bf16[1,1,2048,512]{3,2,1,0:T(8,128)(2,1)} %param.10) | copy-start | bytes 6291460
  6.5 63.5 %all-gather.3.cloned.1.call-start = ((), (), s32[]{:S(2)}) async-start(), calls=%async_computation.1 | async-start | bytes 1081344 | tf_op jit(solution)/shard_map/all_gather | solution.py:73
  6.5 66.1 %collective-permute-start = (bf16[1,1,2048,512]{3,2,1,0:T(8,128)(2,1)}, bf16[1,1,2048,512]{3,2,1,0:T(8,128)(2,1)}, u32[]{:S(2)}, u32[]{:S(2)}) collective-permute-start(bf16[1,1,2048,512]{3,2,1,0:T(8,128)(2,1)} %param.10), channel_id=1, source_target_pairs={{0,4},{4,8},{8,12},{12,16},{16,20},{20,24},{24,28},{28,0},{1,5},{5... | collective-permute-start | bytes 6291464 | tf_op jit(solution)/shard_map/ppermute | solution.py:13
  7.0 65.6 %collective-permute-start.1 = (bf16[1,1,2048,512]{3,2,1,0:T(8,128)(2,1)}, bf16[1,1,2048,512]{3,2,1,0:T(8,128)(2,1)}, u32[]{:S(2)}, u32[]{:S(2)}) collective-permute-start(bf16[1,1,2048,512]{3,2,1,0:T(8,128)(2,1)} %param.10), channel_id=1, source_target_pairs={{4,0},{8,4},{12,8},{16,12},{20,16},{24,20},{28,24},{0,28},{5,1},{9... | collective-permute-start | bytes 6291464 | tf_op jit(solution)/shard_map/ppermute | solution.py:16
  18.4 43.1 %all-to-all-start = ((f32[32,1,1024]{2,1,0:T(1,128)}), f32[32,1,1024]{2,1,0:T(1,128)S(1)}, u32[]{:S(2)}, u32[]{:S(2)}) async-start(f32[32,1,1024]{2,1,0:T(1,128)} %reshape.99), calls=%async_computation | async-start | bytes 262144 | tf_op jit(solution)/shard_map/all_to_all | solution.py:67
Sparse Core Ops, SparseCore 0:
  12.9 57.1 all-gather.2
where the time goes:
time: 92.2 us; the launch traced here: 91.9 us
  waiting for transfers between devices  33.9 us (37%)
  matrix products  29.4 us (32%)
  between operations  14.8 us (16%)
  starting transfers between devices  9.07 us (10%)
  other arithmetic  2.67 us (3%)
  local copies, waits for them, and re-layouts  1.99 us (2%)
    all_to_all x1, waiting for transfers between devices, on_device(): lax.all_to_all(coupled_blocks, ('row', 'col'), split_axis=0, concat_axis=...  27 us
    dot_general x3, matrix products, contract(): lax.dot_general(tile, values, (((0,), (0,)), ((), ())), preferred_element...  24.8 us
    all_gather x1, waiting for transfers between devices, on_device(): lax.all_gather(coefficient_table[None], ('row', 'col'), axis=0, tiled=True)  6.89 us
    all_to_all x1, starting transfers between devices, on_device(): lax.all_to_all(coupled_blocks, ('row', 'col'), split_axis=0, concat_axis=...  5.65 us
    ppermute x1, starting transfers between devices, with_halo(): lax.ppermute(lax.slice_in_dim(block, 0, width, axis=dim), axis, backward)  2.93 us
    dot_general x1, matrix products, on_device(): lax.dot_general(onehot, masked.reshape(slot_count, rank_dimension * rank_...  2.04 us
  transfers between devices with their start and end apart: 4, of which 2 were waited for; matrix products, arithmetic and copies ran while one was open for 24% of the time, Pallas kernels for 0%

commit v1 on v0

v1 whole, which is shorter than its diff:
```python
import functools

import jax
import jax.numpy as jnp
from jax import lax
from jax.experimental import pallas as pl
from jax.experimental.pallas import tpu as pltpu
from jax.sharding import PartitionSpec as P

MESH = pl.DeviceIdType.MESH
CORES = 2
MROWS = 256


def contract(a, b):
    return lax.dot_general(
        a, b, (((0,), (0,)), ((), ())), preferred_element_type=jnp.float32
    )


def kernel(
    rows, cols, chunks,
    near_ref, count_ref, x_ref, rb_ref, cb_ref, coup_ref, tgt_ref, rank_ref, self_hbm, side_hbm,
    out_ref,
    self_v, side_v, above, below, acc, table, cbuf, rec,
    tile_sem, out_sem, up_s, up_r, dn_s, dn_r, a_s, a_r, b_s, b_r, c_s, c_r, k_s, k_r,
):
    total = rows * cols
    chips = rows // CORES
    leaf, width = x_ref.shape
    slots, flat = coup_ref.shape
    rank = rb_ref.shape[1]
    row, col = lax.axis_index("row"), lax.axis_index("col")
    core, chip = lax.rem(row, CORES), row // CORES
    me = row * cols + col
    my_slot = (core * cols + col) * chips + chip

    def place(j):
        return (j // cols, lax.rem(j, cols))

    barrier = pltpu.get_barrier_semaphore()

    def greet(k, carry):
        pl.semaphore_signal(
            barrier, inc=1, device_id=place(lax.rem(me + k, total)), device_id_type=MESH
        )
        return carry

    lax.fori_loop(1, total, greet, 0)
    load_self = pltpu.make_async_copy(self_hbm, self_v, tile_sem.at[0])
    load_side = pltpu.make_async_copy(side_hbm, side_v, tile_sem.at[1])
    load_self.start()
    load_side.start()

    table[my_slot] = contract(rb_ref[...], x_ref[...]).astype(jnp.bfloat16)
    position = lax.broadcasted_iota(jnp.int32, (slots, flat), 1)
    slot = lax.broadcasted_iota(jnp.int32, (slots, flat), 0)
    ranks = rank_ref[...]
    keep = (position // rank < ranks) & (position % rank < ranks) & (slot < count_ref[0, 0])
    masked = jnp.where(keep, coup_ref[...].astype(jnp.float32), 0.0).astype(jnp.bfloat16)
    onehot = (lax.broadcasted_iota(jnp.int32, (total, slots), 0) == tgt_ref[...]).astype(
        jnp.float32
    ).astype(jnp.bfloat16)
    sums = jnp.dot(onehot, masked, preferred_element_type=jnp.float32)
    for j in range(total):
        cbuf[j] = sums[j : j + 1, :]
    rec[my_slot] = cbuf[me]

    pl.semaphore_wait(barrier, total - 1)

    def send(src, dst, s, r, to):
        return pltpu.make_async_remote_copy(
            src_ref=src, dst_ref=dst, send_sem=s, recv_sem=r, device_id=to, device_id_type=MESH
        )

    stage_a = []
    for k in range(1, chips):
        other = lax.rem(chip + k, chips)
        copy = send(
            table.at[my_slot], table.at[my_slot], a_s.at[k], a_r.at[k], (other * CORES + core, col)
        )
        copy.start()
        stage_a.append(copy)

    def couple(k):
        j = lax.rem(me + k, total)
        return send(cbuf.at[j], rec.at[my_slot], k_s.at[k], k_r.at[k], place(j))

    def couple_start(k, carry):
        couple(k).start()
        return carry

    lax.fori_loop(1, total, couple_start, 0)

    depth = leaf // chunks
    after, before = lax.rem(row + 1, rows), lax.rem(row + rows - 1, rows)
    ups, downs = [], []
    for c in range(chunks):
        part = pl.ds(c * depth, depth)
        up = send(x_ref.at[part], above.at[part], up_s.at[c], up_r.at[c], (after, col))
        down = send(x_ref.at[part], below.at[part], dn_s.at[c], dn_r.at[c], (before, col))
        up.start()
        down.start()
        ups.append(up)
        downs.append(down)

    tiles = leaf // MROWS

    def own(m, carry):
        at = pl.ds(pl.multiple_of(m * MROWS, MROWS), MROWS)
        acc[at, :] = contract(self_v[:, at], x_ref[...])
        return carry

    load_self.wait()
    lax.fori_loop(0, tiles // 4, own, 0)

    for copy in stage_a:
        copy.wait()
    group = core * cols + col
    stage_b = []
    mine = table.at[pl.ds(group * chips, chips)]
    for k in range(1, cols):
        copy = send(mine, mine, b_s.at[k], b_r.at[k], (row, lax.rem(col + k, cols)))
        copy.start()
        stage_b.append(copy)
    lax.fori_loop(tiles // 4, tiles, own, 0)

    for copy in stage_b:
        copy.wait()
    half = table.at[pl.ds(core * (cols * chips), cols * chips)]
    stage_c = send(half, half, c_s, c_r, (chip * CORES + (1 - core), col))
    stage_c.start()

    side = near_ref[0, 0]
    from_above = jnp.where(side == -1, 1.0, 0.0).astype(jnp.float32)
    from_below = jnp.where(side == 1, 1.0, 0.0).astype(jnp.float32)
    load_side.wait()

    def near(c, finish):
        ups[c].wait()
        downs[c].wait()
        part = pl.ds(c * depth, depth)
        values = (
            above[part, :].astype(jnp.float32) * from_above
            + below[part, :].astype(jnp.float32) * from_below
        ).astype(jnp.bfloat16)

        def body(m, carry):
            at = pl.ds(pl.multiple_of(m * MROWS, MROWS), MROWS)
            acc[at, :] += contract(side_v[part, at], values)
            if finish:
                pltpu.make_async_copy(acc.at[at], out_ref.at[at], out_sem.at[m]).start()
            return carry

        lax.fori_loop(0, tiles, body, 0)

    near(0, False)
    near(1, False)
    stage_c.wait()

    def couple_wait(k, carry):
        couple(k).wait()
        return carry

    lax.fori_loop(1, total, couple_wait, 0)
    batch = 8
    diagonal = (
        lax.broadcasted_iota(jnp.int32, (rank, flat), 1) // rank
        == lax.broadcasted_iota(jnp.int32, (rank, flat), 0)
    )
    fold = (
        lax.broadcasted_iota(jnp.int32, (flat, rank), 0) % rank
        == lax.broadcasted_iota(jnp.int32, (flat, rank), 1)
    ).astype(jnp.float32).astype(jnp.bfloat16)

    def gather(g, dual):
        spread = [
            jnp.where(diagonal, rec[g * batch + s], 0.0).astype(jnp.bfloat16) for s in range(batch)
        ]
        blocks = jnp.dot(
            jnp.concatenate(spread, axis=0), fold, preferred_element_type=jnp.float32
        ).astype(jnp.bfloat16)
        coefs = table[pl.ds(g * batch, batch)].reshape(batch * rank, width)
        return dual + contract(blocks, coefs)

    dual = lax.fori_loop(0, total // batch, gather, jnp.zeros((rank, width), jnp.float32))
    dual = dual.astype(jnp.bfloat16)

    def distant(m, carry):
        at = pl.ds(pl.multiple_of(m * MROWS, MROWS), MROWS)
        acc[at, :] += jnp.dot(cb_ref[at, :], dual, preferred_element_type=jnp.float32)
        return carry

    lax.fori_loop(0, tiles, distant, 0)
    for c in range(2, chunks):
        near(c, c == chunks - 1)

    def drain(m, carry):
        at = pl.ds(pl.multiple_of(m * MROWS, MROWS), MROWS)
        pltpu.make_async_copy(acc.at[at], out_ref.at[at], out_sem.at[m]).wait()
        return carry

    lax.fori_loop(0, tiles, drain, 0)


def on_device(
    rows, cols, residual, self_tiles, side_tiles, row_cluster_basis, column_cluster_basis,
    couplings, near_side, adm_targets, adm_ranks, adm_count,
):
    leaf, width = residual.shape[2:]
    slots, rank = couplings.shape[2:4]
    total, chips, chunks = rows * cols, rows // CORES, 8
    vmem = pl.BlockSpec(memory_space=pltpu.VMEM)
    smem = pl.BlockSpec(memory_space=pltpu.SMEM)
    anywhere = pl.BlockSpec(memory_space=pl.ANY)
    dma = pltpu.SemaphoreType.DMA
    gradient = pl.pallas_call(
        functools.partial(kernel, rows, cols, chunks),
        out_shape=jax.ShapeDtypeStruct((leaf, width), jnp.float32),
        in_specs=[smem, smem] + [vmem] * 6 + [anywhere] * 2,
        out_specs=anywhere,
        scratch_shapes=[
            pltpu.VMEM((leaf, leaf), jnp.bfloat16),
            pltpu.VMEM((leaf, leaf), jnp.bfloat16),
            pltpu.VMEM((leaf, width), jnp.bfloat16),
            pltpu.VMEM((leaf, width), jnp.bfloat16),
            pltpu.VMEM((leaf, width), jnp.float32),
            pltpu.VMEM((total, rank, width), jnp.bfloat16),
            pltpu.VMEM((total, 1, rank * rank), jnp.float32),
            pltpu.VMEM((total, 1, rank * rank), jnp.float32),
            dma((2,)), dma((leaf // MROWS,)),
            dma((chunks,)), dma((chunks,)), dma((chunks,)), dma((chunks,)),
            dma((chips,)), dma((chips,)), dma((cols,)), dma((cols,)), dma, dma,
            dma((total,)), dma((total,)),
        ],
        compiler_params=pltpu.CompilerParams(
            collective_id=0, has_side_effects=True, vmem_limit_bytes=60 * 1024 * 1024
        ),
    )(
        near_side, adm_count, residual[0, 0], row_cluster_basis[0, 0], column_cluster_basis[0, 0],
        couplings.reshape(slots, rank * rank), adm_targets.reshape(1, slots),
        adm_ranks.reshape(slots, 1), self_tiles[0, 0], side_tiles[0, 0],
    )
    return gradient[None, None]


def solution(mesh):
    placed = (
        P("row", "col", None, None),
        P("row", "col", None, None),
        P("row", "col", None, None),
        P("row", "col", None, None),
        P("row", "col", None, None),
        P("row", "col", None, None, None),
        P("row", "col"),
        P("row", "col", None),
        P("row", "col", None),
        P("row", "col"),
    )
    return jax.shard_map(
        functools.partial(on_device, mesh.shape["row"], mesh.shape["col"]),
        mesh=mesh,
        in_specs=placed,
        out_specs=P("row", "col", None, None),
        check_vma=False,
    )
```

time: 92.2 us -> 75.3 us (0.82)
  Pallas kernels: 0 us -> 62.2 us
  waiting for transfers between devices: 33.9 us -> 0 us
  matrix products: 29.4 us -> 0 us
  between operations: 14.8 us -> 1.31 us
  local copies, waits for them, and re-layouts: 1.99 us -> 11.5 us
  starting transfers between devices: 9.07 us -> 0 us
  other arithmetic: 2.67 us -> 0 us
    pallas_call x0 -> x1, Pallas kernels: none -> 62.2 us  [on_device(): pl.pallas_call(functools.partial(kernel, rows, cols, chunks), out_shape=j...]
    dot_general x6 -> x0, matrix products: 29.4 us -> none  [the longest x3 24.8 us: contract(): lax.dot_general(tile, values, (((0,), (0,)), ((), ())), preferred_element...]
    all_to_all x1 -> x0, waiting for transfers between devices: 27 us -> none  [on_device(): lax.all_to_all(coupled_blocks, ('row', 'col'), split_axis=0, concat_axis=...]
    unnamed x6 -> x3, local copies, waits for them, and re-layouts: 1.08 us -> 8.45 us
    all_gather x1 -> x0, waiting for transfers between devices: 6.89 us -> none  [on_device(): lax.all_gather(coefficient_table[None], ('row', 'col'), axis=0, tiled=True)]
    all_to_all x1 -> x0, starting transfers between devices: 5.65 us -> none  [on_device(): lax.all_to_all(coupled_blocks, ('row', 'col'), split_axis=0, concat_axis=...]
    ppermute x2 -> x0, starting transfers between devices: 3.42 us -> none  [the longest x1 2.93 us: with_halo(): lax.ppermute(lax.slice_in_dim(block, 0, width, axis=dim), axis, backward)]
    reshape x0 -> x2, local copies, waits for them, and re-layouts: none -> 3.07 us  [the longest x1 1.72 us: on_device(): couplings.reshape(slots, rank * rank)]
  transfers between devices with their start and end apart: 4 -> 0, of which waited for: 2 -> 0; matrix products, arithmetic and copies ran while one was open for 24% -> 0% of each run, Pallas kernels for 0% -> 0%
where the time goes in v1:
time: 75.3 us; the launch traced here: 75 us
  Pallas kernels  62.2 us (83%)
  local copies, waits for them, and re-layouts  11.5 us (15%)
  between operations  1.31 us (2%)
    pallas_call x1, Pallas kernels, on_device(): pl.pallas_call(functools.partial(kernel, rows, cols, chunks), out_shape=j...  62.2 us
    unnamed x3, local copies, waits for them, and re-layouts  8.45 us
    reshape x1, local copies, waits for them, and re-layouts, on_device(): couplings.reshape(slots, rank * rank)  1.72 us

profile of v1, /device:TPU:0, one launch (start us, length us, event | category | flops | bytes accessed | tf_op | source)
XLA Modules:
  0.0 75.0 jit_solution(12967260011184823106)
XLA Ops:
  1.3 1.3 %copy.18.rank_ref = s32[64,1]{1,0:T(8,128)} copy(s32[64,1]{0,1:T(1,128)} %bitcast.16) | data formatting | bytes 512 | tf_op jit(solution)/shard_map/reshape | solution.py:242
  2.6 1.7 %copy.17.coup_ref = bf16[64,1024]{1,0:T(8,128)(2,1)} copy(bf16[64,1024]{0,1:T(8,128)(2,1)} %bitcast.15) | data formatting | bytes 262144 | tf_op jit(solution)/shard_map/reshape | solution.py:241
  4.4 1.9 %copy.15 = bf16[1,1,2048,32]{3,2,1,0:T(8,128)(2,1)} copy(bf16[1,1,2048,32]{2,3,1,0:T(8,128)(2,1)} %param.13) | data formatting | bytes 262144 | tf_op args[3]
  6.3 1.9 %copy.16 = bf16[1,1,2048,32]{3,2,1,0:T(8,128)(2,1)} copy(bf16[1,1,2048,32]{2,3,1,0:T(8,128)(2,1)} %param.14) | data formatting | bytes 262144 | tf_op args[4]
  8.2 62.2 %shard_map.100 = f32[2048,512]{1,0:T(8,128)} custom-call(s32[1,1]{1,0:T(1,128)S(6)} %copy.20.near_ref, s32[1,1]{1,0:T(1,128)S(6)} %copy.21.count_ref, bf16[2048,512]{1,0:T(8,128)(2,1)} %bitcast.14, bf16[2048,32]{1,0:T(8,128)(2,1)} %bitcast.12, bf16[2048,32]{1,0:T(8,128)(2,1)} %bitcast.13, bf16[64,1024]{1,0:T(8,128)(2,1)} %copy.17.coup_ref, ...), custom_call_target="tpu_custom_call" | custom-call | tf_op jit(solution)/shard_map/pallas_call | solution.py:217
  70.4 4.6 %copy.22 = f32[1,1,2048,512]{3,2,1,0:T(8,128)} copy(f32[1,1,2048,512]{3,2,1,0:T(8,128)} %bitcast.9) | data formatting | bytes 8388608

commit v2 on v1

--- a/solution.py
+++ b/solution.py
@@ -20,16 +20,16 @@
 
 def kernel(
     rows, cols, chunks,
-    near_ref, count_ref, x_ref, rb_ref, cb_ref, coup_ref, tgt_ref, rank_ref, self_hbm, side_hbm,
+    near_ref, count_ref, tgt_ref, rank_ref, x_hbm, rb_hbm, cb_hbm, coup_hbm, self_hbm, side_hbm,
     out_ref,
-    self_v, side_v, above, below, acc, table, cbuf, rec,
+    x_ref, rb_ref, cb_ref, coup_ref, self_v, side_v, above, below, acc, table, cbuf, rec,
     tile_sem, out_sem, up_s, up_r, dn_s, dn_r, a_s, a_r, b_s, b_r, c_s, c_r, k_s, k_r,
 ):
     total = rows * cols
     chips = rows // CORES
     leaf, width = x_ref.shape
-    slots, flat = coup_ref.shape
-    rank = rb_ref.shape[1]
+    flat, slots = coup_ref.shape
+    rank = rb_ref.shape[0]
     row, col = lax.axis_index("row"), lax.axis_index("col")
     core, chip = lax.rem(row, CORES), row // CORES
     me = row * cols + col
@@ -46,25 +46,42 @@
         )
         return carry
 
+    pairs = (
+        (rb_hbm, rb_ref), (coup_hbm, coup_ref), (x_hbm, x_ref), (cb_hbm, cb_ref),
+        (self_hbm, self_v), (side_hbm, side_v),
+    )
+    loads = [
+        pltpu.make_async_copy(src, dst, tile_sem.at[i]) for i, (src, dst) in enumerate(pairs)
+    ]
+    for load in loads:
+        load.start()
+    load_rb, load_coup, load_x, load_cb, load_self, load_side = loads
     lax.fori_loop(1, total, greet, 0)
-    load_self = pltpu.make_async_copy(self_hbm, self_v, tile_sem.at[0])
-    load_side = pltpu.make_async_copy(side_hbm, side_v, tile_sem.at[1])
-    load_self.start()
-    load_side.start()
-
-    table[my_slot] = contract(rb_ref[...], x_ref[...]).astype(jnp.bfloat16)
-    position = lax.broadcasted_iota(jnp.int32, (slots, flat), 1)
-    slot = lax.broadcasted_iota(jnp.int32, (slots, flat), 0)
+
+    load_coup.wait()
+    position = lax.broadcasted_iota(jnp.int32, (flat, slots), 0)
+    slot = lax.broadcasted_iota(jnp.int32, (flat, slots), 1)
     ranks = rank_ref[...]
-    keep = (position // rank < ranks) & (position % rank < ranks) & (slot < count_ref[0, 0])
+    keep = (
+        (lax.div(position, rank) < ranks)
+        & (lax.rem(position, rank) < ranks)
+        & (slot < count_ref[0, 0])
+    )
     masked = jnp.where(keep, coup_ref[...].astype(jnp.float32), 0.0).astype(jnp.bfloat16)
     onehot = (lax.broadcasted_iota(jnp.int32, (total, slots), 0) == tgt_ref[...]).astype(
         jnp.float32
     ).astype(jnp.bfloat16)
-    sums = jnp.dot(onehot, masked, preferred_element_type=jnp.float32)
+    sums = lax.dot_general(
+        onehot, masked, (((1,), (1,)), ((), ())), preferred_element_type=jnp.float32
+    )
     for j in range(total):
         cbuf[j] = sums[j : j + 1, :]
     rec[my_slot] = cbuf[me]
+    load_rb.wait()
+    load_x.wait()
+    table[my_slot] = jnp.dot(
+        rb_ref[...], x_ref[...], preferred_element_type=jnp.float32
+    ).astype(jnp.bfloat16)
 
     pl.semaphore_wait(barrier, total - 1)
 
@@ -165,11 +182,11 @@
     lax.fori_loop(1, total, couple_wait, 0)
     batch = 8
     diagonal = (
-        lax.broadcasted_iota(jnp.int32, (rank, flat), 1) // rank
+        lax.div(lax.broadcasted_iota(jnp.int32, (rank, flat), 1), rank)
         == lax.broadcasted_iota(jnp.int32, (rank, flat), 0)
     )
     fold = (
-        lax.broadcasted_iota(jnp.int32, (flat, rank), 0) % rank
+        lax.rem(lax.broadcasted_iota(jnp.int32, (flat, rank), 0), rank)
         == lax.broadcasted_iota(jnp.int32, (flat, rank), 1)
     ).astype(jnp.float32).astype(jnp.bfloat16)
 
@@ -188,9 +205,10 @@
 
     def distant(m, carry):
         at = pl.ds(pl.multiple_of(m * MROWS, MROWS), MROWS)
-        acc[at, :] += jnp.dot(cb_ref[at, :], dual, preferred_element_type=jnp.float32)
-        return carry
-
+        acc[at, :] += contract(cb_ref[:, at], dual)
+        return carry
+
+    load_cb.wait()
     lax.fori_loop(0, tiles, distant, 0)
     for c in range(2, chunks):
         near(c, c == chunks - 1)
@@ -217,9 +235,13 @@
     gradient = pl.pallas_call(
         functools.partial(kernel, rows, cols, chunks),
         out_shape=jax.ShapeDtypeStruct((leaf, width), jnp.float32),
-        in_specs=[smem, smem] + [vmem] * 6 + [anywhere] * 2,
+        in_specs=[smem, smem, vmem, vmem] + [anywhere] * 6,
         out_specs=anywhere,
         scratch_shapes=[
+            pltpu.VMEM((leaf, width), jnp.bfloat16),
+            pltpu.VMEM((rank, leaf), jnp.bfloat16),
+            pltpu.VMEM((rank, leaf), jnp.bfloat16),
+            pltpu.VMEM((rank * rank, slots), jnp.bfloat16),
             pltpu.VMEM((leaf, leaf), jnp.bfloat16),
             pltpu.VMEM((leaf, leaf), jnp.bfloat16),
             pltpu.VMEM((leaf, width), jnp.bfloat16),
@@ -228,7 +250,7 @@
             pltpu.VMEM((total, rank, width), jnp.bfloat16),
             pltpu.VMEM((total, 1, rank * rank), jnp.float32),
             pltpu.VMEM((total, 1, rank * rank), jnp.float32),
-            dma((2,)), dma((leaf // MROWS,)),
+            dma((6,)), dma((leaf // MROWS,)),
             dma((chunks,)), dma((chunks,)), dma((chunks,)), dma((chunks,)),
             dma((chips,)), dma((chips,)), dma((cols,)), dma((cols,)), dma, dma,
             dma((total,)), dma((total,)),
@@ -237,9 +259,9 @@
             collective_id=0, has_side_effects=True, vmem_limit_bytes=60 * 1024 * 1024
         ),
     )(
-        near_side, adm_count, residual[0, 0], row_cluster_basis[0, 0], column_cluster_basis[0, 0],
-        couplings.reshape(slots, rank * rank), adm_targets.reshape(1, slots),
-        adm_ranks.reshape(slots, 1), self_tiles[0, 0], side_tiles[0, 0],
+        near_side, adm_count, adm_targets.reshape(1, slots), adm_ranks.reshape(1, slots),
+        residual[0, 0], row_cluster_basis[0, 0].T, column_cluster_basis[0, 0].T,
+        couplings.reshape(slots, rank * rank).T, self_tiles[0, 0], side_tiles[0, 0],
     )
     return gradient[None, None]
 

time: 75.3 us -> 67.2 us (0.89)
  local copies, waits for them, and re-layouts: 11.5 us -> 4.64 us
  Pallas kernels: 62.2 us -> 61 us
    unnamed x3 -> x1, local copies, waits for them, and re-layouts: 8.45 us -> 4.64 us
    reshape x2 -> x0, local copies, waits for them, and re-layouts: 3.07 us -> none  [the longest x1 1.72 us: on_device(): couplings.reshape(slots, rank * rank)]
    pallas_call x1, Pallas kernels: 62.2 us -> 61 us  [on_device(): pl.pallas_call(functools.partial(kernel, rows, cols, chunks), out_shape=j...]
where the time goes in v2:
time: 67.2 us; the launch traced here: 67 us
  Pallas kernels  61 us (91%)
  local copies, waits for them, and re-layouts  4.64 us (7%)
  between operations  1.3 us (2%)
    pallas_call x1, Pallas kernels, on_device(): pl.pallas_call(functools.partial(kernel, rows, cols, chunks), out_shape=j...  61 us
    unnamed x1, local copies, waits for them, and re-layouts  4.64 us

profile of v2, /device:TPU:0, one launch (start us, length us, event | category | flops | bytes accessed | tf_op | source)
XLA Modules:
  0.0 67.0 jit_solution(5637327454909040840)
XLA Ops:
  1.3 61.0 %shard_map.100 = f32[2048,512]{1,0:T(8,128)} custom-call(s32[1,1]{1,0:T(1,128)S(6)} %copy.12.near_ref, s32[1,1]{1,0:T(1,128)S(6)} %copy.13.count_ref, s32[1,64]{1,0:T(1,128)} %bitcast.22, s32[1,64]{1,0:T(1,128)} %bitcast.23, bf16[2048,512]{1,0:T(8,128)(2,1)} %bitcast.18, bf16[32,2048]{1,0:T(8,128)(2,1)} %bitcast.20, bf16[32,2048]{1,0:T(8,128)(2,1)} %bitcast.21, ...), custom_call_target="tpu_custom_call" | custom-call | tf_op jit(solution)/shard_map/pallas_call | solution.py:235
  62.3 4.6 %copy.14 = f32[1,1,2048,512]{3,2,1,0:T(8,128)} copy(f32[1,1,2048,512]{3,2,1,0:T(8,128)} %bitcast.15) | data formatting | bytes 8388608
